TPU v7x, 32 devices: a whole 2x2x4 slice. The times are simulated.
32 devices in a mesh: sp: 8 (over z, x), tp: 4 (over y, core).
Axes of the slice: x: 2, y: 2, z: 4, core: 2. Of those that a mesh axis runs over, the one named last changes fastest.
Arguments:
- prefill_keys: bfloat16 [2, 8, 512, 8, 128], P(None, None, 'sp', 'tp'), may hold values from -6 to 6
- prefill_values: bfloat16 [2, 8, 512, 8, 128], P(None, None, 'sp', 'tp'), may hold values from -6 to 6
- prompt_lengths: int32 [8], replicated, may hold values from 1 to 512, 2048 in all
- destination: int32 [8], replicated, may hold values from 0 to 7, each once
- page_table: int32 [8, 32], P('sp'), may hold values from 0 to 31, as said below
- queries: bfloat16 [2, 8, 64, 128], P(None, 'sp', 'tp'), may hold values from -6 to 6
Outputs:
- key_pages: bfloat16 [2, 256, 16, 8, 128], P(None, 'sp', None, 'tp')
- value_pages: bfloat16 [2, 256, 16, 8, 128], P(None, 'sp', None, 'tp')
- attended: bfloat16 [2, 8, 64, 128], P(None, 'sp')
Inputs may be any that keep to these rules, and one draw needn't show every extreme that they name: `destination`: each slot is named by exactly one prompt; slot s is held by sp index s // 1. `page_table`: the rows of the 1 slots of one sp index together name each of that index's 1 times 32 local pool pages exactly once.
All inputs are finite; a program needn't handle non-finite values.
Results may differ from a plain program's by a relative error of at most 0.0085.
Values may be sent and summed in bfloat16 or wider, within the bound.
A program may use at most 128 MiB of HBM per device.

v0:
```python
import jax
import jax.numpy as jnp
from jax import lax
from jax.sharding import PartitionSpec as P


def local(prefill_keys, prefill_values, prompt_lengths, destination, page_table, queries):
    layers = prefill_keys.shape[0]
    prompts = prefill_keys.shape[1]
    heads_here = prefill_keys.shape[3]
    head_size = prefill_keys.shape[4]
    prompt_ids = jnp.arange(prompts, dtype=jnp.int32)
    chooser = destination[None, :] == prompt_ids[:, None]
    holder = jnp.sum(jnp.where(chooser, prompt_ids[None, :], 0), axis=1).astype(jnp.int32)
    chooser_mat = chooser.astype(jnp.bfloat16)
    sorted_keys = jnp.einsum(
        "sp,lptkd->lstkd", chooser_mat, prefill_keys, preferred_element_type=jnp.float32
    ).astype(jnp.bfloat16)
    sorted_values = jnp.einsum(
        "sp,lptkd->lstkd", chooser_mat, prefill_values, preferred_element_type=jnp.float32
    ).astype(jnp.bfloat16)
    seq_keys, seq_values = (
        lax.all_to_all(sorted_keys, "sp", split_axis=1, concat_axis=2, tiled=True),
        lax.all_to_all(sorted_values, "sp", split_axis=1, concat_axis=2, tiled=True),
    )
    slots_here = page_table.shape[0]
    pages_each = page_table.shape[1]
    max_len = seq_keys.shape[2]
    page_size = max_len // pages_each
    first_slot = lax.axis_index("sp") * slots_here
    my_holder = lax.dynamic_slice_in_dim(holder, first_slot, slots_here)
    my_len = jnp.sum(
        jnp.where(prompt_ids[None, :] == my_holder[:, None], prompt_lengths[None, :], 0), axis=1
    ).astype(jnp.int32)
    positions = jnp.arange(max_len, dtype=jnp.int32)
    inside = positions[None, :] < my_len[:, None]
    seq_keys = jnp.where(inside[None, :, :, None, None], seq_keys, 0).astype(seq_keys.dtype)
    seq_values = jnp.where(inside[None, :, :, None, None], seq_values, 0).astype(seq_values.dtype)
    local_pages = slots_here * pages_each
    block_shape = (layers, local_pages, page_size, heads_here, head_size)
    page_order = page_table.reshape(-1)
    placing = (page_order[:, None] == jnp.arange(local_pages, dtype=jnp.int32)[None, :]).astype(
        jnp.bfloat16
    )
    key_blocks = seq_keys.reshape(block_shape)
    value_blocks = seq_values.reshape(block_shape)
    key_pages = jnp.einsum(
        "iq,liokd->lqokd", placing, key_blocks, preferred_element_type=jnp.float32
    ).astype(jnp.bfloat16)
    value_pages = jnp.einsum(
        "iq,liokd->lqokd", placing, value_blocks, preferred_element_type=jnp.float32
    ).astype(jnp.bfloat16)
    seq_shape = (layers, slots_here, max_len, heads_here, head_size)
    read_keys = (
        jnp.einsum("iq,lqokd->liokd", placing, key_pages, preferred_element_type=jnp.float32)
        .astype(jnp.bfloat16)
        .reshape(seq_shape)
    )
    read_values = (
        jnp.einsum("iq,lqokd->liokd", placing, value_pages, preferred_element_type=jnp.float32)
        .astype(jnp.bfloat16)
        .reshape(seq_shape)
    )
    query_heads = queries.shape[2]
    groups = query_heads // heads_here
    score_scale = head_size ** (-0.5)
    grouped = queries.reshape(layers, slots_here, heads_here, groups, head_size)
    scores = (
        jnp.einsum("lpkgd,lptkd->lpkgt", grouped, read_keys, preferred_element_type=jnp.float32)
        * score_scale
    )
    scores = jnp.where(inside[None, :, None, None, :], scores, -1e30)
    weights = jax.nn.softmax(scores, axis=-1)
    output = jnp.einsum("lpkgt,lptkd->lpkgd", weights, read_values.astype(jnp.float32))
    output = output.reshape(layers, slots_here, query_heads, head_size).astype(jnp.bfloat16)
    attended = lax.all_gather(output, "tp", axis=2, tiled=True)
    return (key_pages, value_pages, attended)


def solution(mesh):
    placed = (
        P(None, None, "sp", "tp", None),
        P(None, None, "sp", "tp", None),
        P(),
        P(),
        P("sp", None),
        P(None, "sp", "tp", None),
    )
    return jax.shard_map(
        local,
        mesh=mesh,
        in_specs=placed,
        out_specs=(
            P(None, "sp", None, "tp", None),
            P(None, "sp", None, "tp", None),
            P(None, "sp", None, None),
        ),
        check_vma=False,
    )
```

profile of v0, /device:TPU:0, one launch (start us, length us, event | category | flops | bytes accessed | tf_op | source)
XLA Modules:
  0.0 56.7 jit_solution(9429967539409540372)
XLA Ops:
  0.6 0.0 copy-start
  0.6 1.0 %copy-done = bf16[2,8,64,2,128]{4,3,2,1,0:T(2,128)(2,1)S(1)} copy-done((bf16[2,8,64,2,128]{4,3,2,1,0:T(2,128)(2,1)S(1)}, bf16[2,8,64,2,128]{4,3,2,1,0:T(2,128)(2,1)}, u32[]{:S(2)}) %copy-start) | copy-done | bytes 524312
  1.7 1.1 %fusion = bf16[2,8,64,2,128]{4,1,3,2,0:T(8,128)(2,1)S(1)} fusion(bf16[2,8,64,2,128]{4,3,2,1,0:T(2,128)(2,1)S(1)} %copy-done, s32[8]{0:T(128)} %param.9), kind=kOutput, calls=%fused_computation.6 | convolution fusion | flops 4456512 | bytes 1048608 | tf_op jit(solution)/shard_map/sp,lptkd->lstkd/dot_general | solution.py:16
  2.7 1.3 %copy.30 = bf16[2,8,64,2,128]{4,3,2,0,1:T(2,128)(2,1)} copy(bf16[2,8,64,2,128]{4,1,3,2,0:T(8,128)(2,1)S(1)} %fusion) | data formatting | bytes 1048576 | tf_op jit(solution)/shard_map/convert_element_type | solution.py:18
  4.0 0.0 copy-start.1
  4.0 0.0 copy-start.4
  4.0 7.4 %all-to-all-start = ((bf16[2,8,64,2,128]{4,3,2,0,1:T(2,128)(2,1)}), bf16[2,8,64,2,128]{4,3,2,0,1:T(2,128)(2,1)S(1)}, u32[]{:S(2)}, u32[]{:S(2)}) async-start(bf16[2,8,64,2,128]{4,3,2,0,1:T(2,128)(2,1)} %copy.30), calls=%async_computation | async-start | bytes 1048576 | tf_op jit(solution)/shard_map/all_to_all | solution.py:23
  11.4 0.0 copy-done.1
  11.4 0.0 copy-done.4
  11.4 0.4 fusion.1
  11.8 1.3 %copy.35 = bf16[2,8,64,2,128]{4,3,2,0,1:T(2,128)(2,1)} copy(bf16[2,8,64,2,128]{4,1,3,2,0:T(8,128)(2,1)S(1)} %fusion.1) | data formatting | bytes 1048576 | tf_op jit(solution)/shard_map/convert_element_type | solution.py:21
  13.1 12.8 %all-to-all-done = bf16[2,8,64,2,128]{4,3,2,0,1:T(2,128)(2,1)S(1)} async-done(((bf16[2,8,64,2,128]{4,3,2,0,1:T(2,128)(2,1)}), bf16[2,8,64,2,128]{4,3,2,0,1:T(2,128)(2,1)S(1)}, u32[]{:S(2)}, u32[]{:S(2)}) %all-to-all-start) | async-done | bytes 524320 | tf_op jit(solution)/shard_map/all_to_all | solution.py:23
  25.9 3.6 %all-to-all-start.1 = ((bf16[2,8,64,2,128]{4,3,2,0,1:T(2,128)(2,1)}), bf16[2,8,64,2,128]{4,3,2,0,1:T(2,128)(2,1)S(1)}, u32[]{:S(2)}, u32[]{:S(2)}) async-start(bf16[2,8,64,2,128]{4,3,2,0,1:T(2,128)(2,1)} %copy.35), calls=%async_computation.1 | async-start | bytes 1048576 | tf_op jit(solution)/shard_map/all_to_all | solution.py:24
  29.5 0.1 select_reduce_fusion
  29.7 0.6 %dynamic_slice.3 = s32[1]{0:T(128)} dynamic-slice(s32[8]{0:T(128)S(1)} %select_reduce_fusion, s32[]{:T(128)S(6)} %select_n.34), dynamic_slice_sizes={1} | dynamic-slice | bytes 12 | tf_op jit(solution)/shard_map/dynamic_slice | solution.py:31
  30.2 0.0 copy-start.5
  30.2 0.7 %copy-done.5 = s32[8]{0:T(128)S(1)} copy-done((s32[8]{0:T(128)S(1)}, s32[8]{0:T(128)}, u32[]{:S(2)}) %copy-start.5) | copy-done | bytes 56
  30.9 1.3 %fusion.32 = s32[]{:T(128)} fusion(s32[8]{0:T(128)S(1)} %copy-done.5, s32[]{:T(128)} %bitcast), kind=kLoop, calls=%fused_computation.43 | loop fusion | flops 23 | bytes 40 | tf_op jit(solution)/shard_map/reduce_sum | solution.py:32
  32.2 0.6 %iota_compare_fusion.2 = pred[512]{0:T(512)(128)(4,1)S(1)} fusion(s32[]{:T(128)} %fusion.32), kind=kLoop, calls=%fused_computation.39 | loop fusion | flops 512 | bytes 516 | tf_op jit(solution)/shard_map/lt | solution.py:36
  32.8 0.7 %add_compare_fusion = pred[32,16]{1,0:T(8,128)(4,1)S(1)} fusion(s32[]{:T(128)} %fusion.32), kind=kLoop, calls=%fused_computation.29 | loop fusion | flops 1536 | bytes 516 | tf_op jit(solution)/shard_map/lt | solution.py:36
  33.5 0.1 copy.31
  33.6 10.6 %all-to-all-done.1 = bf16[2,8,64,2,128]{4,3,2,0,1:T(2,128)(2,1)S(1)} async-done(((bf16[2,8,64,2,128]{4,3,2,0,1:T(2,128)(2,1)}), bf16[2,8,64,2,128]{4,3,2,0,1:T(2,128)(2,1)S(1)}, u32[]{:S(2)}, u32[]{:S(2)}) %all-to-all-start.1) | async-done | bytes 524320 | tf_op jit(solution)/shard_map/all_to_all | solution.py:24
  44.2 0.1 copy.36
  44.3 0.1 broadcast_select_fusion
  44.5 0.0 copy-start.3
  44.5 0.6 %copy-done.3 = s32[1,32]{1,0:T(1,128)S(1)} copy-done((s32[1,32]{1,0:T(1,128)S(1)}, s32[1,32]{1,0:T(1,128)}, u32[]{:S(2)}) %copy-start.3) | copy-done | bytes 152
  45.1 0.4 fusion.2
  45.6 1.2 %copy.42 = bf16[2,32,16,2,128]{4,3,2,1,0:T(2,128)(2,1)} copy(bf16[2,32,16,2,128]{4,1,3,2,0:T(8,128)(2,1)S(1)} %fusion.2) | data formatting | bytes 1048576
  46.8 0.3 fusion.4
  47.1 0.4 fusion.3
  47.5 1.2 %copy.43 = bf16[2,32,16,2,128]{4,3,2,1,0:T(2,128)(2,1)} copy(bf16[2,32,16,2,128]{4,1,3,2,0:T(8,128)(2,1)S(1)} %fusion.3) | data formatting | bytes 1048576
  48.7 0.3 fusion.5
  49.1 0.3 copy.39
  49.4 0.0 copy-start.2
  49.5 0.3 copy.40
  49.8 0.3 copy-done.2
  50.1 0.3 fusion.33
  50.5 0.2 fusion.14
  50.7 0.2 fusion.8
  50.9 5.2 %all_gather.3 = bf16[2,1,64,128]{3,2,1,0:T(8,128)(2,1)S(1)} all-gather(bf16[2,1,16,128]{3,2,1,0:T(8,128)(2,1)S(1)} %fusion.8), channel_id=1, replica_groups=mesh['sp'=8,'tp'=4] {'tp'}, dimensions={2}, use_global_device_ids=true | all-gather | bytes 40960 | tf_op jit(solution)/shard_map/all_gather | solution.py:76
  56.1 0.6 %copy.59 = bf16[2,1,64,128]{3,2,1,0:T(8,128)(2,1)} copy(bf16[2,1,64,128]{3,2,1,0:T(8,128)(2,1)S(1)} %all_gather.3) | data formatting | bytes 65536
Async XLA Ops:
  0.6 1.0 %copy-start = (bf16[2,8,64,2,128]{4,3,2,1,0:T(2,128)(2,1)S(1)}, bf16[2,8,64,2,128]{4,3,2,1,0:T(2,128)(2,1)}, u32[]{:S(2)}) copy-start(bf16[2,8,64,2,128]{4,3,2,1,0:T(2,128)(2,1)} %param.6) | copy-start | bytes 1572868
  4.0 7.4 %copy-start.1 = (bf16[2,8,64,2,128]{4,3,2,1,0:T(2,128)(2,1)S(1)}, bf16[2,8,64,2,128]{4,3,2,1,0:T(2,128)(2,1)}, u32[]{:S(2)}) copy-start(bf16[2,8,64,2,128]{4,3,2,1,0:T(2,128)(2,1)} %param.7) | copy-start | bytes 1572868
  4.0 7.4 %copy-start.4 = (s32[8]{0:T(128)S(1)}, s32[8]{0:T(128)}, u32[]{:S(2)}) copy-start(s32[8]{0:T(128)} %param.9) | copy-start | bytes 100
  4.0 21.9 %all-to-all-start = ((bf16[2,8,64,2,128]{4,3,2,0,1:T(2,128)(2,1)}), bf16[2,8,64,2,128]{4,3,2,0,1:T(2,128)(2,1)S(1)}, u32[]{:S(2)}, u32[]{:S(2)}) async-start(bf16[2,8,64,2,128]{4,3,2,0,1:T(2,128)(2,1)} %copy.30), calls=%async_computation | async-start | bytes 1048576 | tf_op jit(solution)/shard_map/all_to_all | solution.py:23
  25.9 18.3 %all-to-all-start.1 = ((bf16[2,8,64,2,128]{4,3,2,0,1:T(2,128)(2,1)}), bf16[2,8,64,2,128]{4,3,2,0,1:T(2,128)(2,1)S(1)}, u32[]{:S(2)}, u32[]{:S(2)}) async-start(bf16[2,8,64,2,128]{4,3,2,0,1:T(2,128)(2,1)} %copy.35), calls=%async_computation.1 | async-start | bytes 1048576 | tf_op jit(solution)/shard_map/all_to_all | solution.py:24
  30.2 0.7 %copy-start.5 = (s32[8]{0:T(128)S(1)}, s32[8]{0:T(128)}, u32[]{:S(2)}) copy-start(s32[8]{0:T(128)} %param.8) | copy-start | bytes 100
  44.5 0.7 %copy-start.3 = (s32[1,32]{1,0:T(1,128)S(1)}, s32[1,32]{1,0:T(1,128)}, u32[]{:S(2)}) copy-start(s32[1,32]{1,0:T(1,128)} %param.10) | copy-start | bytes 388
  49.4 0.7 %copy-start.2 = (bf16[2,1,16,128]{3,2,1,0:T(8,128)(2,1)S(1)}, bf16[2,1,16,128]{3,2,1,0:T(8,128)(2,1)}, u32[]{:S(2)}) copy-start(bf16[2,1,16,128]{3,2,1,0:T(8,128)(2,1)} %param.11) | copy-start | bytes 24580
where the time goes:
time: 57.1 us; the launch traced here: 56.7 us
  waiting for transfers between devices  23.4 us (41%)
  starting transfers between devices  11 us (19%)
  local copies, waits for them, and re-layouts  9.74 us (17%)
  blocking collectives  5.19 us (9%)
  matrix products  3.54 us (6%)
  other arithmetic  3.03 us (5%)
  between operations  0.76 us (1%)
    all_to_all x1, waiting for transfers between devices, local(): lax.all_to_all(sorted_keys, 'sp', split_axis=1, concat_axis=2, tiled=True)  12.8 us
    all_to_all x1, waiting for transfers between devices, local(): lax.all_to_all(sorted_values, 'sp', split_axis=1, concat_axis=2, tiled=True)  10.6 us
    all_to_all x1, starting transfers between devices, local(): lax.all_to_all(sorted_keys, 'sp', split_axis=1, concat_axis=2, tiled=True)  7.41 us
    unnamed x15, local copies, waits for them, and re-layouts  5.71 us
    all_gather x1, blocking collectives, local(): attended = lax.all_gather(output, 'tp', axis=2, tiled=True)  5.19 us
    all_to_all x1, starting transfers between devices, local(): lax.all_to_all(sorted_values, 'sp', split_axis=1, concat_axis=2, tiled=True)  3.64 us
    lt x2, other arithmetic, local(): inside = positions[None, :] < my_len[:, None]  1.31 us
    reduce_sum x1, other arithmetic, local(): jnp.sum(jnp.where(prompt_ids[None, :] == my_holder[:, None], prompt_lengt...  1.27 us
  transfers between devices with their start and end apart: 2, of which 2 were waited for; matrix products, arithmetic and copies ran while one was open for 9% of the time, Pallas kernels for 0%

commit v1 on v0

--- a/solution.py
+++ b/solution.py
@@ -2,6 +2,20 @@
 import jax.numpy as jnp
 from jax import lax
 from jax.sharding import PartitionSpec as P
+
+
+def page_map(mine, along_axis):
+    chips = lax.axis_size(along_axis)
+    series = [mine]
+    for hop_no in range(chips - 1):
+        series.append(
+            lax.ppermute(series[-1], along_axis, [(b, (b + 1) % chips) for b in range(chips)])
+        )
+    return jnp.roll(
+        jnp.concatenate(series[::-1], axis=2),
+        (lax.axis_index(along_axis) + 1) * mine.shape[2],
+        axis=2,
+    )
 
 
 def local(prefill_keys, prefill_values, prompt_lengths, destination, page_table, queries):
@@ -73,7 +87,7 @@
     weights = jax.nn.softmax(scores, axis=-1)
     output = jnp.einsum("lpkgt,lptkd->lpkgd", weights, read_values.astype(jnp.float32))
     output = output.reshape(layers, slots_here, query_heads, head_size).astype(jnp.bfloat16)
-    attended = lax.all_gather(output, "tp", axis=2, tiled=True)
+    attended = page_map(output, "tp")
     return (key_pages, value_pages, attended)
 
 

time: 57.1 us -> 59.4 us (1.040)
  waiting for transfers between devices: 23.4 us -> 30.2 us
  blocking collectives: 5.19 us -> 0 us
    ppermute x0 -> x3, waiting for transfers between devices: none -> 6.81 us  [page_map(): lax.ppermute(series[-1], along_axis, [(b, (b + 1) % chips) for b in range...]
    all_gather x1 -> x0, blocking collectives: 5.19 us -> none  [local(): attended = lax.all_gather(output, 'tp', axis=2, tiled=True)]
    dynamic_slice x0 -> x1, local copies, waits for them, and re-layouts: none -> 0.63 us  [page_map(): jnp.roll(jnp.concatenate(series[::-1], axis=2), (lax.axis_index(along_axi...]
    unnamed x15 -> x21, local copies, waits for them, and re-layouts: 5.71 us -> 5.14 us
  transfers between devices with their start and end apart: 2 -> 5, of which waited for: 2 -> 5; matrix products, arithmetic and copies ran while one was open for 9% -> 13% of each run, Pallas kernels for 0% -> 0%
where the time goes in v1:
time: 59.4 us; the launch traced here: 58.5 us
  waiting for transfers between devices  30.2 us (51%)
  starting transfers between devices  11.1 us (19%)
  local copies, waits for them, and re-layouts  9.81 us (17%)
  matrix products  3.53 us (6%)
  other arithmetic  3.03 us (5%)
  between operations  0.78 us (1%)
    all_to_all x1, waiting for transfers between devices, local(): lax.all_to_all(sorted_keys, 'sp', split_axis=1, concat_axis=2, tiled=True)  12.8 us
    all_to_all x1, waiting for transfers between devices, local(): lax.all_to_all(sorted_values, 'sp', split_axis=1, concat_axis=2, tiled=True)  10.6 us
    all_to_all x1, starting transfers between devices, local(): lax.all_to_all(sorted_keys, 'sp', split_axis=1, concat_axis=2, tiled=True)  7.41 us
    ppermute x3, waiting for transfers between devices, page_map(): lax.ppermute(series[-1], along_axis, [(b, (b + 1) % chips) for b in range...  6.81 us
    unnamed x21, local copies, waits for them, and re-layouts  5.14 us
    all_to_all x1, starting transfers between devices, local(): lax.all_to_all(sorted_values, 'sp', split_axis=1, concat_axis=2, tiled=True)  3.64 us
    lt x2, other arithmetic, local(): inside = positions[None, :] < my_len[:, None]  1.31 us
    reduce_sum x1, other arithmetic, local(): jnp.sum(jnp.where(prompt_ids[None, :] == my_holder[:, None], prompt_lengt...  1.27 us
  transfers between devices with their start and end apart: 5, of which 5 were waited for; matrix products, arithmetic and copies ran while one was open for 13% of the time, Pallas kernels for 0%

profile of v1, /device:TPU:0, one launch (start us, length us, event | category | flops | bytes accessed | tf_op | source)
XLA Modules:
  0.0 58.5 jit_solution(16001728083668961178)
XLA Ops:
  0.6 0.0 copy-start
  0.6 1.0 %copy-done = bf16[2,8,64,2,128]{4,3,2,1,0:T(2,128)(2,1)S(1)} copy-done((bf16[2,8,64,2,128]{4,3,2,1,0:T(2,128)(2,1)S(1)}, bf16[2,8,64,2,128]{4,3,2,1,0:T(2,128)(2,1)}, u32[]{:S(2)}) %copy-start) | copy-done | bytes 524312
  1.7 1.1 %fusion = bf16[2,8,64,2,128]{4,1,3,2,0:T(8,128)(2,1)S(1)} fusion(bf16[2,8,64,2,128]{4,3,2,1,0:T(2,128)(2,1)S(1)} %copy-done, s32[8]{0:T(128)} %param.9), kind=kOutput, calls=%fused_computation.6 | convolution fusion | flops 4456512 | bytes 1048608 | tf_op jit(solution)/shard_map/sp,lptkd->lstkd/dot_general | solution.py:30
  2.7 1.3 %copy.34 = bf16[2,8,64,2,128]{4,3,2,0,1:T(2,128)(2,1)} copy(bf16[2,8,64,2,128]{4,1,3,2,0:T(8,128)(2,1)S(1)} %fusion) | data formatting | bytes 1048576 | tf_op jit(solution)/shard_map/convert_element_type | solution.py:32
  4.0 0.0 copy-start.1
  4.0 0.0 copy-start.4
  4.0 7.4 %all-to-all-start = ((bf16[2,8,64,2,128]{4,3,2,0,1:T(2,128)(2,1)}), bf16[2,8,64,2,128]{4,3,2,0,1:T(2,128)(2,1)S(1)}, u32[]{:S(2)}, u32[]{:S(2)}) async-start(bf16[2,8,64,2,128]{4,3,2,0,1:T(2,128)(2,1)} %copy.34), calls=%async_computation | async-start | bytes 1048576 | tf_op jit(solution)/shard_map/all_to_all | solution.py:37
  11.4 0.0 copy-done.1
  11.4 0.0 copy-done.4
  11.4 0.4 fusion.1
  11.8 1.3 %copy.39 = bf16[2,8,64,2,128]{4,3,2,0,1:T(2,128)(2,1)} copy(bf16[2,8,64,2,128]{4,1,3,2,0:T(8,128)(2,1)S(1)} %fusion.1) | data formatting | bytes 1048576 | tf_op jit(solution)/shard_map/convert_element_type | solution.py:35
  13.1 12.8 %all-to-all-done = bf16[2,8,64,2,128]{4,3,2,0,1:T(2,128)(2,1)S(1)} async-done(((bf16[2,8,64,2,128]{4,3,2,0,1:T(2,128)(2,1)}), bf16[2,8,64,2,128]{4,3,2,0,1:T(2,128)(2,1)S(1)}, u32[]{:S(2)}, u32[]{:S(2)}) %all-to-all-start) | async-done | bytes 524320 | tf_op jit(solution)/shard_map/all_to_all | solution.py:37
  25.9 3.6 %all-to-all-start.1 = ((bf16[2,8,64,2,128]{4,3,2,0,1:T(2,128)(2,1)}), bf16[2,8,64,2,128]{4,3,2,0,1:T(2,128)(2,1)S(1)}, u32[]{:S(2)}, u32[]{:S(2)}) async-start(bf16[2,8,64,2,128]{4,3,2,0,1:T(2,128)(2,1)} %copy.39), calls=%async_computation.1 | async-start | bytes 1048576 | tf_op jit(solution)/shard_map/all_to_all | solution.py:38
  29.5 0.1 select_reduce_fusion
  29.7 0.6 %dynamic_slice.7 = s32[1]{0:T(128)} dynamic-slice(s32[8]{0:T(128)S(1)} %select_reduce_fusion, s32[]{:T(128)S(6)} %select_n.47), dynamic_slice_sizes={1} | dynamic-slice | bytes 12 | tf_op jit(solution)/shard_map/dynamic_slice | solution.py:45
  30.2 0.0 copy-start.5
  30.2 0.7 %copy-done.5 = s32[8]{0:T(128)S(1)} copy-done((s32[8]{0:T(128)S(1)}, s32[8]{0:T(128)}, u32[]{:S(2)}) %copy-start.5) | copy-done | bytes 56
  30.9 1.3 %fusion.32 = s32[]{:T(128)} fusion(s32[8]{0:T(128)S(1)} %copy-done.5, s32[]{:T(128)} %bitcast), kind=kLoop, calls=%fused_computation.51 | loop fusion | flops 23 | bytes 40 | tf_op jit(solution)/shard_map/reduce_sum | solution.py:46
  32.2 0.6 %iota_compare_fusion.2 = pred[512]{0:T(512)(128)(4,1)S(1)} fusion(s32[]{:T(128)} %fusion.32), kind=kLoop, calls=%fused_computation.47 | loop fusion | flops 512 | bytes 516 | tf_op jit(solution)/shard_map/lt | solution.py:50
  32.8 0.7 %add_compare_fusion = pred[32,16]{1,0:T(8,128)(4,1)S(1)} fusion(s32[]{:T(128)} %fusion.32), kind=kLoop, calls=%fused_computation.37 | loop fusion | flops 1536 | bytes 516 | tf_op jit(solution)/shard_map/lt | solution.py:50
  33.5 0.1 copy.35
  33.6 10.6 %all-to-all-done.1 = bf16[2,8,64,2,128]{4,3,2,0,1:T(2,128)(2,1)S(1)} async-done(((bf16[2,8,64,2,128]{4,3,2,0,1:T(2,128)(2,1)}), bf16[2,8,64,2,128]{4,3,2,0,1:T(2,128)(2,1)S(1)}, u32[]{:S(2)}, u32[]{:S(2)}) %all-to-all-start.1) | async-done | bytes 524320 | tf_op jit(solution)/shard_map/all_to_all | solution.py:38
  44.2 0.1 copy.40
  44.3 0.1 broadcast_select_fusion
  44.5 0.0 copy-start.3
  44.5 0.6 %copy-done.3 = s32[1,32]{1,0:T(1,128)S(1)} copy-done((s32[1,32]{1,0:T(1,128)S(1)}, s32[1,32]{1,0:T(1,128)}, u32[]{:S(2)}) %copy-start.3) | copy-done | bytes 152
  45.1 0.4 fusion.3
  45.6 0.4 fusion.2
  46.0 0.3 fusion.4
  46.3 0.3 copy.43
  46.7 0.3 fusion.5
  47.0 0.0 copy-start.2
  47.1 0.3 copy.44
  47.4 0.3 copy-done.2
  47.7 0.3 fusion.33
  48.1 0.2 fusion.14
  48.3 0.2 fusion.8
  48.5 0.0 collective-permute-start
  48.5 3.1 %collective-permute-done = bf16[2,1,16,128]{3,2,1,0:T(8,128)(2,1)S(1)} collective-permute-done((bf16[2,1,16,128]{3,2,1,0:T(8,128)(2,1)S(1)}, bf16[2,1,16,128]{3,2,1,0:T(8,128)(2,1)S(1)}, u32[]{:S(2)}, u32[]{:S(2)}) %collective-permute-start) | collective-permute-done | bytes 8224 | tf_op jit(solution)/shard_map/ppermute | solution.py:12
  51.6 0.0 collective-permute-start.1
  51.6 3.1 %collective-permute-done.1 = bf16[2,1,16,128]{3,2,1,0:T(8,128)(2,1)S(1)} collective-permute-done((bf16[2,1,16,128]{3,2,1,0:T(8,128)(2,1)S(1)}, bf16[2,1,16,128]{3,2,1,0:T(8,128)(2,1)S(1)}, u32[]{:S(2)}, u32[]{:S(2)}) %collective-permute-start.1) | collective-permute-done | bytes 8224 | tf_op jit(solution)/shard_map/ppermute | solution.py:12
  54.7 0.0 collective-permute-start.2
  54.7 1.2 %copy.48 = bf16[2,32,16,2,128]{4,3,2,1,0:T(2,128)(2,1)} copy(bf16[2,32,16,2,128]{4,1,3,2,0:T(8,128)(2,1)S(1)} %fusion.2) | data formatting | bytes 1048576
  55.9 1.2 %copy.49 = bf16[2,32,16,2,128]{4,3,2,1,0:T(2,128)(2,1)} copy(bf16[2,32,16,2,128]{4,1,3,2,0:T(8,128)(2,1)S(1)} %fusion.3) | data formatting | bytes 1048576
  57.1 0.7 %collective-permute-done.2 = bf16[2,1,16,128]{3,2,1,0:T(8,128)(2,1)S(1)} collective-permute-done((bf16[2,1,16,128]{3,2,1,0:T(8,128)(2,1)S(1)}, bf16[2,1,16,128]{3,2,1,0:T(8,128)(2,1)S(1)}, u32[]{:S(2)}, u32[]{:S(2)}) %collective-permute-start.2) | collective-permute-done | bytes 8224 | tf_op jit(solution)/shard_map/ppermute | solution.py:12
  57.8 0.6 %constant_dynamic-slice_fusion = bf16[2,1,64,128]{3,2,1,0:T(8,128)(2,1)} fusion(bf16[2,1,128,128]{3,2,1,0:T(8,128)(2,1)S(1)} %constant_dynamic-update-slice_fusion, s32[]{:T(128)S(6)} %select_n.54), kind=kLoop, calls=%fused_computation.52 | loop fusion | bytes 65540 | tf_op jit(solution)/shard_map/jit(_roll_dynamic)/dynamic_slice | solution.py:14
  (8 shorter events, 0.1 us)
Async XLA Ops:
  0.6 1.0 %copy-start = (bf16[2,8,64,2,128]{4,3,2,1,0:T(2,128)(2,1)S(1)}, bf16[2,8,64,2,128]{4,3,2,1,0:T(2,128)(2,1)}, u32[]{:S(2)}) copy-start(bf16[2,8,64,2,128]{4,3,2,1,0:T(2,128)(2,1)} %param.6) | copy-start | bytes 1572868
  4.0 7.4 %copy-start.1 = (bf16[2,8,64,2,128]{4,3,2,1,0:T(2,128)(2,1)S(1)}, bf16[2,8,64,2,128]{4,3,2,1,0:T(2,128)(2,1)}, u32[]{:S(2)}) copy-start(bf16[2,8,64,2,128]{4,3,2,1,0:T(2,128)(2,1)} %param.7) | copy-start | bytes 1572868
  4.0 7.4 %copy-start.4 = (s32[8]{0:T(128)S(1)}, s32[8]{0:T(128)}, u32[]{:S(2)}) copy-start(s32[8]{0:T(128)} %param.9) | copy-start | bytes 100
  4.0 21.9 %all-to-all-start = ((bf16[2,8,64,2,128]{4,3,2,0,1:T(2,128)(2,1)}), bf16[2,8,64,2,128]{4,3,2,0,1:T(2,128)(2,1)S(1)}, u32[]{:S(2)}, u32[]{:S(2)}) async-start(bf16[2,8,64,2,128]{4,3,2,0,1:T(2,128)(2,1)} %copy.34), calls=%async_computation | async-start | bytes 1048576 | tf_op jit(solution)/shard_map/all_to_all | solution.py:37
  25.9 18.3 %all-to-all-start.1 = ((bf16[2,8,64,2,128]{4,3,2,0,1:T(2,128)(2,1)}), bf16[2,8,64,2,128]{4,3,2,0,1:T(2,128)(2,1)S(1)}, u32[]{:S(2)}, u32[]{:S(2)}) async-start(bf16[2,8,64,2,128]{4,3,2,0,1:T(2,128)(2,1)} %copy.39), calls=%async_computation.1 | async-start | bytes 1048576 | tf_op jit(solution)/shard_map/all_to_all | solution.py:38
  30.2 0.7 %copy-start.5 = (s32[8]{0:T(128)S(1)}, s32[8]{0:T(128)}, u32[]{:S(2)}) copy-start(s32[8]{0:T(128)} %param.8) | copy-start | bytes 100
  44.5 0.7 %copy-start.3 = (s32[1,32]{1,0:T(1,128)S(1)}, s32[1,32]{1,0:T(1,128)}, u32[]{:S(2)}) copy-start(s32[1,32]{1,0:T(1,128)} %param.10) | copy-start | bytes 388
  47.0 0.7 %copy-start.2 = (bf16[2,1,16,128]{3,2,1,0:T(8,128)(2,1)S(1)}, bf16[2,1,16,128]{3,2,1,0:T(8,128)(2,1)}, u32[]{:S(2)}) copy-start(bf16[2,1,16,128]{3,2,1,0:T(8,128)(2,1)} %param.11) | copy-start | bytes 24580
  48.5 3.1 %collective-permute-start = (bf16[2,1,16,128]{3,2,1,0:T(8,128)(2,1)S(1)}, bf16[2,1,16,128]{3,2,1,0:T(8,128)(2,1)S(1)}, u32[]{:S(2)}, u32[]{:S(2)}) collective-permute-start(bf16[2,1,16,128]{3,2,1,0:T(8,128)(2,1)S(1)} %fusion.8), channel_id=1, source_target_pairs={{0,1},{1,2},{2,3},{3,0},{4,5},{5,6},{6,7},{7,4},{8,9},{9,10},{10,1... | collective-permute-start | bytes 24584 | tf_op jit(solution)/shard_map/ppermute | solution.py:12
  51.6 3.1 %collective-permute-start.1 = (bf16[2,1,16,128]{3,2,1,0:T(8,128)(2,1)S(1)}, bf16[2,1,16,128]{3,2,1,0:T(8,128)(2,1)S(1)}, u32[]{:S(2)}, u32[]{:S(2)}) collective-permute-start(bf16[2,1,16,128]{3,2,1,0:T(8,128)(2,1)S(1)} %collective-permute-done), channel_id=1, source_target_pairs={{0,1},{1,2},{2,3},{3,0},{4,5},{5,6},{6,7},{7,4},{8,9},{9,10},{10,1... | collective-permute-start | bytes 24584 | tf_op jit(solution)/shard_map/ppermute | solution.py:12
  54.7 3.1 %collective-permute-start.2 = (bf16[2,1,16,128]{3,2,1,0:T(8,128)(2,1)S(1)}, bf16[2,1,16,128]{3,2,1,0:T(8,128)(2,1)S(1)}, u32[]{:S(2)}, u32[]{:S(2)}) collective-permute-start(bf16[2,1,16,128]{3,2,1,0:T(8,128)(2,1)S(1)} %collective-permute-done.1), channel_id=1, source_target_pairs={{0,1},{1,2},{2,3},{3,0},{4,5},{5,6},{6,7},{7,4},{8,9},{9,10},{10,1... | collective-permute-start | bytes 24584 | tf_op jit(solution)/shard_map/ppermute | solution.py:12
